TPU v7x, 32 devices: a whole 2x2x4 slice. The times are simulated.
32 devices in a mesh: member: 2 (over y), gy: 4 (over z), gx: 2 (over x), lev: 2 (over core).
Axes of the slice: x: 2, y: 2, z: 4, core: 2. Of those that a mesh axis runs over, the one named last changes fastest.
Arguments:
- level_field: bfloat16 [32, 1536, 1536], P(('member', 'lev'), 'gy', 'gx'), parts along dimension 0, may hold values from -6 to 6
Outputs:
- spectra: float32 [1536, 32, 1536], P(('gy', 'gx'), ('member', 'lev')), parts along dimension 1
- spectra_zone: float32 [1536, 32, 11], P(('gy', 'gx'), ('member', 'lev')), parts along dimension 1
There are 2 independent parts, one for each index of `member`. A program takes and returns all parts, laid end to end along the dimension named above; each array names one. Nothing has to cross between parts.
All inputs are finite; a program needn't handle non-finite values.
Results may differ from a plain program's by a relative error of at most 0.0042.
Values may be sent and summed in bfloat16 or wider, within the bound.
A program may use at most 128 MiB of HBM per device.

v0:
```python
import math

import jax
import jax.numpy as jnp
from jax import lax
from jax.sharding import PartitionSpec as P

NX = 1536
NY = 1536
EXT_ZONE = 11
WAVES = 768


def blend_zone(second_last, last_value, first_value, second_value, zone_count):
    steps = (jnp.arange(zone_count, dtype=jnp.int32) + 1).astype(jnp.float32) / (zone_count + 1.0)
    weight_a = 2.0 * steps**3 - 3.0 * steps**2 + 1.0
    weight_b = steps**3 - 2.0 * steps**2 + steps
    weight_c = -2.0 * steps**3 + 3.0 * steps**2
    weight_d = steps**3 - steps**2
    tangent_scale = zone_count + 1.0
    slope_start = tangent_scale * (last_value - second_last)
    slope_end = tangent_scale * (second_value - first_value)
    return (
        last_value[..., None] * weight_a
        + slope_start[..., None] * weight_b
        + first_value[..., None] * weight_c
        + slope_end[..., None] * weight_d
    )


def make_table(wave_count, length):
    coeff = jnp.arange(2 * wave_count, dtype=jnp.int32)[:, None]
    column = jnp.arange(length, dtype=jnp.int32)[None, :]
    is_cosine = coeff < wave_count
    number = jnp.where(is_cosine, coeff, coeff - wave_count + 1)
    phase = (number * column % length).astype(jnp.float32) * (2.0 * math.pi / length)
    values = jnp.where(is_cosine, jnp.cos(phase), -jnp.sin(phase)) / math.sqrt(length)
    return values.astype(jnp.bfloat16)


def shards(level_field):
    wave_table = make_table(WAVES, NX + EXT_ZONE)
    core_table = wave_table[:, :NX]
    zone_table = wave_table[:, NX:]
    core_rows = lax.all_to_all(level_field, "gx", split_axis=1, concat_axis=2, tiled=True)
    widened = core_rows.astype(jnp.float32)
    zone_cols = blend_zone(
        widened[..., NX - 2], widened[..., NX - 1], widened[..., 0], widened[..., 1], EXT_ZONE
    ).astype(jnp.bfloat16)
    dims = (((1,), (2,)), ((), ()))
    total = lax.dot_general(core_table, core_rows, dims, preferred_element_type=jnp.float32)
    partial_spec = total + lax.dot_general(
        zone_table, zone_cols, dims, preferred_element_type=jnp.float32
    )
    moved = lax.all_to_all(partial_spec, ("gy", "gx"), split_axis=0, concat_axis=2, tiled=True)
    spectra_zone = blend_zone(
        moved[..., NY - 2], moved[..., NY - 1], moved[..., 0], moved[..., 1], EXT_ZONE
    )
    return (moved, spectra_zone)


def solution(mesh):
    return jax.shard_map(
        shards,
        mesh=mesh,
        in_specs=(P(("member", "lev"), "gy", "gx"),),
        out_specs=(
            P(("gy", "gx"), ("member", "lev"), None),
            P(("gy", "gx"), ("member", "lev"), None),
        ),
        check_vma=False,
    )
```

profile of v0, /device:TPU:0, one launch (start us, length us, event | category | flops | bytes accessed | tf_op | source)
XLA Modules:
  0.0 426.6 jit_solution(1554581682853218261)
XLA Ops:
  0.6 7.1 %copy.14 = bf16[8,384,768]{2,0,1:T(8,128)(2,1)} copy(bf16[8,384,768]{2,1,0:T(8,128)(2,1)} %param.1) | data formatting | bytes 9437184 | tf_op args[0]
  7.8 6.0 %all-to-all-start = ((bf16[8,384,768]{2,0,1:T(8,128)(2,1)}), bf16[8,384,768]{2,0,1:T(8,128)(2,1)}, u32[]{:S(2)}, u32[]{:S(2)}) async-start(bf16[8,384,768]{2,0,1:T(8,128)(2,1)} %copy.14), calls=%async_computation | async-start | bytes 9437184 | tf_op jit(solution)/shard_map/all_to_all | solution.py:45
  13.8 46.7 %multiply_convert_fusion = bf16[1536,1547]{1,0:T(8,128)(2,1)} fusion(s32[1536]{0:T(1024)S(1)} %add_select_fusion.1, pred[1536]{0:T(1024)(128)(4,1)S(1)} %iota_compare_fusion), kind=kLoop, calls=%fused_computation.3 | loop fusion | flops 30890496 | bytes 4760064 | tf_op jit(solution)/shard_map/convert_element_type | solution.py:38
  60.5 7.7 %all-to-all-done = bf16[8,384,768]{2,0,1:T(8,128)(2,1)} async-done(((bf16[8,384,768]{2,0,1:T(8,128)(2,1)}), bf16[8,384,768]{2,0,1:T(8,128)(2,1)}, u32[]{:S(2)}, u32[]{:S(2)}) %all-to-all-start) | async-done | bytes 4718624 | tf_op jit(solution)/shard_map/all_to_all | solution.py:45
  68.2 9.4 %copy.23 = bf16[8,2,192,768]{3,1,2,0:T(2,128)(2,1)} copy(bf16[8,2,192,768]{3,0,2,1:T(8,128)(2,1)} %bitcast.1) | data formatting | bytes 9437184 | tf_op jit(solution)/shard_map/all_to_all | solution.py:45
  77.6 0.0 slice-start.2
  77.6 11.3 %all_to_all.29 = bf16[8,192,1536]{2,1,0:T(8,128)(2,1)} reshape(bf16[8,192,2,768]{3,2,1,0:T(2,128)(2,1)} %bitcast.28) | data formatting | bytes 9437184 | tf_op jit(solution)/shard_map/all_to_all | solution.py:45
  88.9 0.0 slice-start.3
  88.9 3.8 convert_element_type.49
  92.7 0.0 slice-start
  92.7 1.8 slice_reduce_fusion.1
  94.5 0.0 slice-done.2
  94.5 0.0 slice-done.3
  94.6 0.0 slice-start.1
  94.6 1.5 fusion.9
  96.1 0.0 slice-done
  96.1 0.0 slice-done.1
  96.1 10.6 %convolution_add_fusion = f32[1536,8,192]{0,2,1:T(8,128)} fusion(f32[1536,8,192]{0,2,1:T(8,128)S(1)} %fusion.9, bf16[8,192,1536]{2,1,0:T(8,128)(2,1)S(1)} %bitcast.27, bf16[1536,1547]{1,0:T(8,128)(2,1)S(1)} %bitcast.30), kind=kOutput, calls=%fused_computation.8 | convolution fusion | flops 7250116608 | bytes 28311552 | tf_op jit(solution)/shard_map/dot_general | solution.py:51
  106.7 12.8 %copy.17 = f32[1536,8,192]{2,1,0:T(8,128)} copy(f32[1536,8,192]{0,2,1:T(8,128)} %convolution_add_fusion) | data formatting | bytes 18874368 | tf_op jit(solution)/shard_map/add | solution.py:52
  119.5 279.9 %all_to_all.36 = f32[1536,8,192]{2,1,0:T(8,128)} all-to-all(f32[1536,8,192]{2,1,0:T(8,128)} %copy.17), channel_id=1, replica_groups=mesh['member'=2,'gy'=4,'gx'=2,'lev'=2] {'gy','gx'}, dimensions={0} | all-to-all | bytes 18874368 | tf_op jit(solution)/shard_map/all_to_all | solution.py:55
  399.4 13.8 %copy.18 = f32[8,192,8,192]{1,2,3,0:T(8,128)} copy(f32[8,192,8,192]{3,2,1,0:T(8,128)} %bitcast.25) | data formatting | bytes 18874368 | tf_op jit(solution)/shard_map/all_to_all | solution.py:55
  413.2 0.8 slice_bitcast_fusion.5
  414.0 11.9 %copy.19 = f32[192,8,1536]{2,1,0:T(8,128)} copy(f32[192,8,1536]{0,1,2:T(8,128)} %bitcast.24) | data formatting | bytes 18874368
  425.9 0.8 multiply_add_fusion
  (6 shorter events, 0.0 us)
Async XLA Ops:
  7.8 60.5 %all-to-all-start = ((bf16[8,384,768]{2,0,1:T(8,128)(2,1)}), bf16[8,384,768]{2,0,1:T(8,128)(2,1)}, u32[]{:S(2)}, u32[]{:S(2)}) async-start(bf16[8,384,768]{2,0,1:T(8,128)(2,1)} %copy.14), calls=%async_computation | async-start | bytes 9437184 | tf_op jit(solution)/shard_map/all_to_all | solution.py:45
  77.6 16.9 %slice-start.2 = ((s8[5111808]{0:T(1024)(128)(4,1)}), s8[917504]{0:T(1024)(128)(4,1)S(1)}, s32[]{:S(2)}) async-start(s8[5111808]{0:T(1024)(128)(4,1)} %bitcast.29), calls=%async_computation.4 | async-start | bytes 1835008
  88.9 5.6 %slice-start.3 = ((s8[5111808]{0:T(1024)(128)(4,1)}), s8[4194304]{0:T(1024)(128)(4,1)S(1)}, s32[]{:S(2)}) async-start(s8[5111808]{0:T(1024)(128)(4,1)} %bitcast.29), calls=%async_computation.5 | async-start | bytes 8388608
  92.7 3.4 slice-start
  94.6 1.5 slice-start.1
where the time goes:
time: 428 us; the launch traced here: 427 us
  blocking collectives  280 us (65%)
  local copies, waits for them, and re-layouts  66.3 us (15%)
  other arithmetic  53.8 us (13%)
  matrix products  12.1 us (3%)
  waiting for transfers between devices  7.74 us (2%)
  starting transfers between devices  5.95 us (1%)
    all_to_all x1, blocking collectives, shards(): lax.all_to_all(partial_spec, ('gy', 'gx'), split_axis=0, concat_axis=2, t...  280 us
    convert_element_type x1, other arithmetic, make_table(): return values.astype(jnp.bfloat16)  46.7 us
    all_to_all x2, local copies, waits for them, and re-layouts, shards(): lax.all_to_all(level_field, 'gx', split_axis=1, concat_axis=2, tiled=True)  20.7 us
    unnamed x10, local copies, waits for them, and re-layouts  19 us
    all_to_all x1, local copies, waits for them, and re-layouts, shards(): lax.all_to_all(partial_spec, ('gy', 'gx'), split_axis=0, concat_axis=2, t...  13.8 us
    add x1, local copies, waits for them, and re-layouts, shards(): total + lax.dot_general(zone_table, zone_cols, dims, preferred_element_ty...  12.8 us
    dot_general x1, matrix products, shards(): lax.dot_general(core_table, core_rows, dims, preferred_element_type=jnp.f...  10.6 us
  transfers between devices with their start and end apart: 1, of which 1 were waited for; matrix products, arithmetic and copies ran while one was open for 11% of the time, Pallas kernels for 0%

commit v1 on v0

v1 whole, which is shorter than its diff:
```python
import functools
import math

import jax
import jax.numpy as jnp
from jax import lax
from jax.experimental import pallas as pl
from jax.experimental.pallas import tpu as pltpu
from jax.sharding import PartitionSpec as P

EXT_ZONE = 11
LANES = 128
NT = (((1,), (1,)), ((), ()))
MESH = pl.DeviceIdType.MESH


def blend_weights(zone_count):
    steps = (jnp.arange(zone_count, dtype=jnp.int32) + 1).astype(jnp.float32) / (zone_count + 1.0)
    weight_a = 2.0 * steps**3 - 3.0 * steps**2 + 1.0
    weight_b = steps**3 - 2.0 * steps**2 + steps
    weight_c = -2.0 * steps**3 + 3.0 * steps**2
    weight_d = steps**3 - steps**2
    return weight_a, weight_b, weight_c, weight_d


def blend_zone(second_last, last_value, first_value, second_value, zone_count):
    weight_a, weight_b, weight_c, weight_d = blend_weights(zone_count)
    tangent_scale = zone_count + 1.0
    slope_start = tangent_scale * (last_value - second_last)
    slope_end = tangent_scale * (second_value - first_value)
    return (
        last_value[..., None] * weight_a
        + slope_start[..., None] * weight_b
        + first_value[..., None] * weight_c
        + slope_end[..., None] * weight_d
    )


def wave_factors(coeff0, group, column, wave_count, length):
    number0 = jnp.where(coeff0 < wave_count, coeff0, coeff0 - wave_count + 1)
    scale = 2.0 * math.pi / length
    phase0 = (number0[:, None] * column[None, :] % length).astype(jnp.float32) * scale
    cos0, sin0 = jnp.cos(phase0), jnp.sin(phase0)
    is_cosine = (coeff0 < wave_count)[:, None]
    p, q = jnp.where(is_cosine, cos0, -sin0), jnp.where(is_cosine, sin0, cos0)
    step = jnp.arange(group, dtype=jnp.int32)
    phase = (step[:, None] * column[None, :] % length).astype(jnp.float32) * scale
    norm = 1.0 / math.sqrt(length)
    return p, q, jnp.cos(phase) * norm, jnp.sin(phase) * norm


def kernel(n_gx, n_gy, field_ref, edge_ref, table_ref, ztable_ref, weight_ref,
           out_ref, out_edge_ref, xgot, xedge, send, esend, xs, xr, es, er, zs, zr, ts, tr):
    levels, rows, cols = field_ref.shape
    bands = table_ref.shape[2]
    me_x, me_y = lax.axis_index("gx"), lax.axis_index("gy")

    def peer_x(shift):
        return {"gx": lax.rem(me_x + n_gx - shift, n_gx)}

    def peer_y(shift):
        return {"gy": lax.rem(me_y + shift, n_gy)}

    barrier = pltpu.get_barrier_semaphore()
    for shift in range(1, n_gx):
        pl.semaphore_signal(barrier, inc=1, device_id=peer_x(shift), device_id_type=MESH)
    for shift in range(1, n_gy):
        pl.semaphore_signal(barrier, inc=1, device_id=peer_y(shift), device_id_type=MESH)
    pl.semaphore_wait(barrier, n_gx + n_gy - 2)

    def edge_x(shift):
        return pltpu.make_async_remote_copy(
            src_ref=edge_ref, dst_ref=xedge.at[shift - 1], send_sem=es.at[shift - 1],
            recv_sem=er.at[shift - 1], device_id=peer_x(shift), device_id_type=MESH)

    def rows_x(shift, level):
        return pltpu.make_async_remote_copy(
            src_ref=field_ref.at[level], dst_ref=xgot.at[shift - 1, level],
            send_sem=xs.at[shift - 1, level], recv_sem=xr.at[shift - 1, level],
            device_id=peer_x(shift), device_id_type=MESH)

    def edge_y(shift):
        return pltpu.make_async_remote_copy(
            src_ref=esend.at[shift - 1], dst_ref=out_edge_ref.at[shift], send_sem=ts.at[shift - 1],
            recv_sem=tr.at[shift - 1], device_id=peer_y(shift), device_id_type=MESH)

    def spec_y(shift, level):
        return pltpu.make_async_remote_copy(
            src_ref=send.at[shift - 1, level], dst_ref=out_ref.at[shift, level],
            send_sem=zs.at[shift - 1, level], recv_sem=zr.at[shift - 1, level],
            device_id=peer_y(shift), device_id_type=MESH)

    for shift in range(1, n_gx):
        edge_x(shift).start()

    @pl.loop(0, levels)
    def _(level):
        for shift in range(1, n_gx):
            rows_x(shift, level).start()

    tail = (cols - 1) // LANES * LANES

    def zone_of(parts):
        first = second = last = before = 0.0
        for at, part in enumerate(parts):
            owner = lax.rem(me_x + at, n_gx)
            is_first = jnp.where(owner == 0, 1.0, 0.0)
            is_last = jnp.where(owner == n_gx - 1, 1.0, 0.0)
            head = part[:, :min(LANES, cols)].astype(jnp.float32)
            rear = part[:, tail:].astype(jnp.float32)
            first += is_first * head[:, 0:1]
            second += is_first * head[:, 1:2]
            before += is_last * rear[:, cols - 2 - tail:cols - 1 - tail]
            last += is_last * rear[:, cols - 1 - tail:cols - tail]
        tangent = EXT_ZONE + 1.0
        zone = (last * weight_ref[0:1, :] + (tangent * (last - before)) * weight_ref[1:2, :]
                + first * weight_ref[2:3, :] + (tangent * (second - first)) * weight_ref[3:4, :])
        return zone.astype(jnp.bfloat16)

    def dot(a, b):
        return lax.dot_general(a, b, NT, preferred_element_type=jnp.float32)

    for shift in range(1, n_gx):
        edge_x(shift).wait_recv()
    parts = [edge_ref[...]] + [xedge[at] for at in range(n_gx - 1)]
    zone = zone_of(parts)
    for shift in range(n_gy):
        total = dot(zone, ztable_ref[shift])
        for at, part in enumerate(parts):
            total += dot(part, table_ref[at, shift])
        if shift == 0:
            out_edge_ref[0] = total
        else:
            esend[shift - 1] = total
            edge_y(shift).start()

    merged = bands % 16 == 0

    @pl.loop(0, levels)
    def _(level):
        for shift in range(1, n_gx):
            rows_x(shift, level).wait_recv()
        parts = [field_ref[level]] + [xgot[at, level] for at in range(n_gx - 1)]
        zone = zone_of(parts)
        if merged:
            size = n_gy * bands
            total = dot(ztable_ref[...].reshape(size, LANES), zone)
            for at, part in enumerate(parts):
                total += dot(table_ref[at].reshape(size, cols), part)
            pieces = [total[s * bands:(s + 1) * bands] for s in range(n_gy)]
        else:
            pieces = []
            for shift in range(n_gy):
                total = dot(ztable_ref[shift], zone)
                for at, part in enumerate(parts):
                    total += dot(table_ref[at, shift], part)
                pieces.append(total)
        for shift in range(n_gy):
            piece = pieces[shift].astype(jnp.bfloat16)
            if shift == 0:
                out_ref[0, level] = piece
            else:
                send[shift - 1, level] = piece
        for shift in range(1, n_gy):
            spec_y(shift, level).start()

    for shift in range(1, n_gx):
        edge_x(shift).wait_send()
    for shift in range(1, n_gy):
        edge_y(shift).wait()

    @pl.loop(0, levels)
    def _(level):
        for shift in range(1, n_gx):
            rows_x(shift, level).wait_send()
        for shift in range(1, n_gy):
            spec_y(shift, level).wait()


def make_body(mesh):
    n_gx, n_gy = mesh.shape["gx"], mesh.shape["gy"]

    def body(field):
        levels, rows, cols = field.shape
        nx, ny = cols * n_gx, rows * n_gy
        length = nx + EXT_ZONE
        me_x, me_y = lax.axis_index("gx"), lax.axis_index("gy")
        bands = nx // (n_gx * n_gy)
        assert (nx // 2) % bands == 0
        group = 16 if bands % 16 == 0 else bands

        at = jnp.arange(nx + LANES, dtype=jnp.int32)
        column = jnp.where(at < nx, (at + me_x * cols) % nx, at)
        shift_at = jnp.arange(n_gy, dtype=jnp.int32)[:, None]
        coeff = ((me_y + shift_at) % n_gy) * (n_gx * bands) + me_x * bands
        coeff = (coeff + jnp.arange(0, bands, group, dtype=jnp.int32)[None, :]).reshape(-1)
        factors = wave_factors(coeff, group, column, nx // 2, length)
        p, q, c, s = lax.optimization_barrier(factors)

        def expand(lo, hi):
            full = p[:, None, lo:hi] * c[None, :, lo:hi] - q[:, None, lo:hi] * s[None, :, lo:hi]
            return full.astype(jnp.bfloat16).reshape(n_gy, bands, hi - lo)

        table = jnp.stack([expand(i * cols, (i + 1) * cols) for i in range(n_gx)])
        ztable = expand(nx, nx + LANES)
        ztable = jnp.where(jnp.arange(LANES) < EXT_ZONE, ztable, jnp.zeros_like(ztable))
        weights = jnp.pad(jnp.stack(blend_weights(EXT_ZONE)), ((0, 4), (0, LANES - EXT_ZONE)))
        edge = jnp.concatenate([field[:, :2], field[:, rows - 2:]], axis=1)
        edge = edge.transpose(1, 0, 2).reshape(4 * levels, cols)

        vmem = pl.BlockSpec(memory_space=pltpu.VMEM)
        dma = pltpu.SemaphoreType.DMA
        xs, ys = n_gx - 1, n_gy - 1
        got, edge_got = pl.pallas_call(
            functools.partial(kernel, n_gx, n_gy),
            out_shape=(
                jax.ShapeDtypeStruct((n_gy, levels, bands, rows), jnp.bfloat16),
                jax.ShapeDtypeStruct((n_gy, 4 * levels, bands), jnp.float32),
            ),
            in_specs=[vmem] * 5,
            out_specs=(vmem, vmem),
            scratch_shapes=[
                pltpu.VMEM((xs, levels, rows, cols), jnp.bfloat16),
                pltpu.VMEM((xs, 4 * levels, cols), jnp.bfloat16),
                pltpu.VMEM((ys, levels, bands, rows), jnp.bfloat16),
                pltpu.VMEM((ys, 4 * levels, bands), jnp.float32),
                dma((xs, levels)), dma((xs, levels)), dma((xs,)), dma((xs,)),
                dma((ys, levels)), dma((ys, levels)), dma((ys,)), dma((ys,)),
            ],
            compiler_params=pltpu.CompilerParams(collective_id=0, has_side_effects=True),
        )(field, edge, table, ztable, weights)

        edge_got = edge_got.reshape(n_gy, 4, levels, bands)
        low = lax.dynamic_index_in_dim(edge_got, me_y, 0, keepdims=False)
        high = lax.dynamic_index_in_dim(edge_got, (me_y + 1) % n_gy, 0, keepdims=False)
        low, high = low.transpose(0, 2, 1), high.transpose(0, 2, 1)
        spectra_zone = blend_zone(high[2], high[3], low[0], low[1], EXT_ZONE)

        spectra = jnp.zeros((bands, levels, ny), jnp.float32)
        for shift in range(n_gy):
            full = got[shift].transpose(1, 0, 2).astype(jnp.float32)
            source = (me_y + n_gy - shift) % n_gy
            spectra = lax.dynamic_update_slice(spectra, full, (0, 0, source * rows))
        return spectra, spectra_zone

    return body


def solution(mesh):
    return jax.shard_map(
        make_body(mesh),
        mesh=mesh,
        in_specs=(P(("member", "lev"), "gy", "gx"),),
        out_specs=(
            P(("gy", "gx"), ("member", "lev"), None),
            P(("gy", "gx"), ("member", "lev"), None),
        ),
        check_vma=False,
    )
```

time: 428 us -> 162 us (0.38)
  blocking collectives: 280 us -> 0 us
  Pallas kernels: 0 us -> 127 us
  local copies, waits for them, and re-layouts: 66.3 us -> 21.2 us
  other arithmetic: 53.8 us -> 12.3 us
  matrix products: 12.1 us -> 0 us
  waiting for transfers between devices: 7.74 us -> 0 us
  starting transfers between devices: 5.95 us -> 0 us
    all_to_all x1 -> x0, blocking collectives: 280 us -> none  [shards(): lax.all_to_all(partial_spec, ('gy', 'gx'), split_axis=0, concat_axis=2, t...]
    pallas_call x0 -> x1, Pallas kernels: none -> 127 us  [body(): pl.pallas_call(functools.partial(kernel, n_gx, n_gy), out_shape=(jax.Shap...]
    convert_element_type x2 -> x4, other arithmetic: 50.5 us -> 6.51 us  [the longest x1 5.52 us: body(): full = got[shift].transpose(1, 0, 2).astype(jnp.float32)]
    all_to_all x3 -> x0, local copies, waits for them, and re-layouts: 34.5 us -> none  [the longest x2 20.7 us: shards(): lax.all_to_all(level_field, 'gx', split_axis=1, concat_axis=2, tiled=True)]
    unnamed x10 -> x4, local copies, waits for them, and re-layouts: 19 us -> 4.22 us
    dynamic_update_slice x0 -> x4, local copies, waits for them, and re-layouts: none -> 13.2 us  [body(): spectra = lax.dynamic_update_slice(spectra, full, (0, 0, source * rows))]
    add x1, local copies, waits for them, and re-layouts: 12.8 us -> 0.09 us  [body(): coeff + jnp.arange(0, bands, group, dtype=jnp.int32)[None, :]]
    dot_general x2 -> x0, matrix products: 12.1 us -> none  [the longest x1 10.6 us: shards(): lax.dot_general(core_table, core_rows, dims, preferred_element_type=jnp.f...]
  transfers between devices with their start and end apart: 1 -> 0, of which waited for: 1 -> 0; matrix products, arithmetic and copies ran while one was open for 11% -> 0% of each run, Pallas kernels for 0% -> 0%
where the time goes in v1:
time: 162 us; the launch traced here: 161 us
  Pallas kernels  127 us (78%)
  local copies, waits for them, and re-layouts  21.2 us (13%)
  other arithmetic  12.3 us (8%)
    pallas_call x1, Pallas kernels, body(): pl.pallas_call(functools.partial(kernel, n_gx, n_gy), out_shape=(jax.Shap...  127 us
    dynamic_update_slice x4, local copies, waits for them, and re-layouts, body(): spectra = lax.dynamic_update_slice(spectra, full, (0, 0, source * rows))  13.2 us
    convert_element_type x1, other arithmetic, body(): full = got[shift].transpose(1, 0, 2).astype(jnp.float32)  5.52 us
    unnamed x4, local copies, waits for them, and re-layouts  4.22 us

profile of v1, /device:TPU:0, one launch (start us, length us, event | category | flops | bytes accessed | tf_op | source)
XLA Modules:
  0.0 161.1 jit_solution(4292737103615597285)
XLA Ops:
  0.7 0.1 broadcast_add_fusion
  0.7 0.1 add.270
  0.9 1.4 fusion.6
  2.3 0.5 sine_multiply_fusion
  2.7 0.1 fusion.31
  2.8 0.5 subtract_convert_fusion.1
  3.3 0.5 subtract_convert_fusion
  3.7 1.6 pad_maximum_fusion.table_ref
  5.4 0.1 subtract_convert_fusion.2
  5.4 0.7 bitcast_select_fusion.ztable_ref
  6.2 0.6 select_maximum_fusion.weight_ref
  6.8 1.0 fusion.30
  7.8 0.1 maximum_bitcast_fusion
  7.8 0.6 copy.13
  8.4 126.8 %shard_map.30 = (bf16[4,8,192,384]{3,2,1,0:T(8,128)(2,1)}, f32[4,32,192]{2,1,0:T(8,128)}) custom-call(bf16[8,384,768]{2,1,0:T(8,128)(2,1)} %field_ref.1, bf16[32,768]{1,0:T(8,128)(2,1)} %bitcast.62, bf16[2,4,192,768]{3,2,1,0:T(8,128)(2,1)} %pad_maximum_fusion.table_ref, bf16[4,192,128]{2,1,0:T(8,128)(2,1)} %bitcast_select_fusion.ztable_ref, ...), custom_call_target="tpu_custom_call" | custom-call | tf_op jit(solution)/shard_map/pallas_call | solution.py:214
  135.3 0.8 dynamic-slice_bitcast_fusion.1
  136.1 0.8 multiply_add_fusion
  136.9 5.5 %convert_bitcast_fusion = (f32[192,8,384]{2,0,1:T(8,128)S(1)}, f32[192,8,384]{2,0,1:T(8,128)}, f32[192,8,384]{2,0,1:T(8,128)}, f32[192,8,384]{2,0,1:T(8,128)}) fusion(bf16[4,8,192,384]{3,2,1,0:T(8,128)(2,1)} %get-tuple-element.12), kind=kLoop, calls=%fused_computation.1 | loop fusion | flops 2359296 | bytes 14155776 | tf_op jit(solution)/shard_map/convert_element_type | solution.py:241
  142.4 0.0 copy-start
  142.4 1.2 broadcast_in_dim.18
  143.6 0.5 copy-done
  144.1 1.6 copy_dynamic-update-slice_fusion.3
  145.7 0.0 copy-start.1
  145.7 3.7 %copy-done.1 = f32[192,8,1536]{2,1,0:T(8,128)} copy-done((f32[192,8,1536]{2,1,0:T(8,128)}, f32[192,8,1536]{2,1,0:T(8,128)S(1)}, u32[]{:S(2)}) %copy-start.1) | copy-done | bytes 9437208
  149.4 4.4 %copy_dynamic-update-slice_fusion.2 = f32[192,8,1536]{2,1,0:T(8,128)} fusion(f32[192,8,1536]{2,1,0:T(8,128)} %copy-done.1, s32[]{:T(128)S(6)} %select_n.112, f32[192,8,384]{2,0,1:T(8,128)} %get-tuple-element.16), kind=kLoop, calls=%fused_computation.7 | loop fusion | bytes 4718596 | tf_op jit(solution)/shard_map/dynamic_update_slice | solution.py:243
  153.9 4.4 %copy_dynamic-update-slice_fusion.1 = f32[192,8,1536]{2,1,0:T(8,128)} fusion(f32[192,8,1536]{2,1,0:T(8,128)} %copy_dynamic-update-slice_fusion.2, s32[]{:T(128)S(6)} %select_n.114, f32[192,8,384]{2,0,1:T(8,128)} %get-tuple-element.15), kind=kLoop, calls=%fused_computation.6 | loop fusion | bytes 4718596 | tf_op jit(solution)/shard_map/dynamic_update_slice | solution.py:243
  158.3 2.8 %copy_dynamic-update-slice_fusion = f32[192,8,1536]{2,1,0:T(8,128)} fusion(f32[192,8,1536]{2,1,0:T(8,128)} %copy_dynamic-update-slice_fusion.1, s32[]{:T(128)S(6)} %select_n.116, f32[192,8,384]{2,0,1:T(8,128)S(1)} %get-tuple-element.14), kind=kLoop, calls=%fused_computation.5 | loop fusion | bytes 4718596 | tf_op jit(solution)/shard_map/dynamic_update_slice | solution.py:243
  (19 shorter events, 0.1 us)
Async XLA Ops:
  142.4 1.7 %copy-start = (f32[192,8,384]{2,0,1:T(8,128)S(1)}, f32[192,8,384]{2,0,1:T(8,128)}, u32[]{:S(2)}) copy-start(f32[192,8,384]{2,0,1:T(8,128)} %get-tuple-element.17) | copy-start | bytes 7077892
  145.7 3.7 %copy-start.1 = (f32[192,8,1536]{2,1,0:T(8,128)}, f32[192,8,1536]{2,1,0:T(8,128)S(1)}, u32[]{:S(2)}) copy-start(f32[192,8,1536]{2,1,0:T(8,128)S(1)} %copy_dynamic-update-slice_fusion.3) | copy-start | bytes 28311556

commit v2 on v1

--- a/solution.py
+++ b/solution.py
@@ -81,12 +81,12 @@
 
     def edge_y(shift):
         return pltpu.make_async_remote_copy(
-            src_ref=esend.at[shift - 1], dst_ref=out_edge_ref.at[shift], send_sem=ts.at[shift - 1],
+            src_ref=esend.at[shift - 1], dst_ref=out_edge_ref.at[me_y], send_sem=ts.at[shift - 1],
             recv_sem=tr.at[shift - 1], device_id=peer_y(shift), device_id_type=MESH)
 
     def spec_y(shift, level):
         return pltpu.make_async_remote_copy(
-            src_ref=send.at[shift - 1, level], dst_ref=out_ref.at[shift, level],
+            src_ref=send.at[shift - 1, level], dst_ref=out_ref.at[me_y, level],
             send_sem=zs.at[shift - 1, level], recv_sem=zr.at[shift - 1, level],
             device_id=peer_y(shift), device_id_type=MESH)
 
@@ -129,7 +129,7 @@
         for at, part in enumerate(parts):
             total += dot(part, table_ref[at, shift])
         if shift == 0:
-            out_edge_ref[0] = total
+            out_edge_ref[me_y] = total
         else:
             esend[shift - 1] = total
             edge_y(shift).start()
@@ -158,7 +158,7 @@
         for shift in range(n_gy):
             piece = pieces[shift].astype(jnp.bfloat16)
             if shift == 0:
-                out_ref[0, level] = piece
+                out_ref[me_y, level] = piece
             else:
                 send[shift - 1, level] = piece
         for shift in range(1, n_gy):
@@ -231,16 +231,11 @@
         )(field, edge, table, ztable, weights)
 
         edge_got = edge_got.reshape(n_gy, 4, levels, bands)
-        low = lax.dynamic_index_in_dim(edge_got, me_y, 0, keepdims=False)
-        high = lax.dynamic_index_in_dim(edge_got, (me_y + 1) % n_gy, 0, keepdims=False)
+        low, high = edge_got[0], edge_got[n_gy - 1]
         low, high = low.transpose(0, 2, 1), high.transpose(0, 2, 1)
         spectra_zone = blend_zone(high[2], high[3], low[0], low[1], EXT_ZONE)
 
-        spectra = jnp.zeros((bands, levels, ny), jnp.float32)
-        for shift in range(n_gy):
-            full = got[shift].transpose(1, 0, 2).astype(jnp.float32)
-            source = (me_y + n_gy - shift) % n_gy
-            spectra = lax.dynamic_update_slice(spectra, full, (0, 0, source * rows))
+        spectra = got.transpose(2, 1, 0, 3).reshape(bands, levels, ny).astype(jnp.float32)
         return spectra, spectra_zone
 
     return body

time: 162 us -> 171 us (1.056)
  local copies, waits for them, and re-layouts: 21.2 us -> 28 us
    convert_element_type x0 -> x2, local copies, waits for them, and re-layouts: none -> 25.4 us  [body(): got.transpose(2, 1, 0, 3).reshape(bands, levels, ny).astype(jnp.float32)]
    dynamic_update_slice x4 -> x0, local copies, waits for them, and re-layouts: 13.2 us -> none  [body(): spectra = lax.dynamic_update_slice(spectra, full, (0, 0, source * rows))]
    unnamed x4 -> x0, local copies, waits for them, and re-layouts: 4.22 us -> none
    convert_element_type x1, other arithmetic: 5.52 us -> 7.25 us  [body(): got.transpose(2, 1, 0, 3).reshape(bands, levels, ny).astype(jnp.float32)]
where the time goes in v2:
time: 171 us; the launch traced here: 170 us
  Pallas kernels  127 us (74%)
  local copies, waits for them, and re-layouts  28 us (16%)
  other arithmetic  14 us (8%)
    pallas_call x1, Pallas kernels, body(): pl.pallas_call(functools.partial(kernel, n_gx, n_gy), out_shape=(jax.Shap...  127 us
    convert_element_type x2, local copies, waits for them, and re-layouts, body(): got.transpose(2, 1, 0, 3).reshape(bands, levels, ny).astype(jnp.float32)  25.4 us
    convert_element_type x1, other arithmetic, body(): got.transpose(2, 1, 0, 3).reshape(bands, levels, ny).astype(jnp.float32)  7.25 us

profile of v2, /device:TPU:0, one launch (start us, length us, event | category | flops | bytes accessed | tf_op | source)
XLA Modules:
  0.0 169.6 jit_solution(10702481830228561007)
XLA Ops:
  0.7 0.1 broadcast_add_fusion
  0.7 0.1 add.223
  0.9 0.6 select_maximum_fusion.weight_ref
  1.5 1.0 fusion.30
  2.5 0.1 maximum_bitcast_fusion
  2.6 0.6 copy.7
  3.2 0.5 sine_multiply_fusion
  3.6 1.4 fusion.6
  5.1 0.1 fusion.31
  5.2 0.1 subtract_convert_fusion.2
  5.2 0.7 bitcast_select_fusion.ztable_ref
  6.0 0.5 subtract_convert_fusion.1
  6.4 0.5 subtract_convert_fusion
  6.9 1.6 pad_maximum_fusion.table_ref
  8.5 126.8 %shard_map.30 = (bf16[4,8,192,384]{3,2,1,0:T(8,128)(2,1)}, f32[4,32,192]{2,1,0:T(8,128)}) custom-call(bf16[8,384,768]{2,1,0:T(8,128)(2,1)} %field_ref.1, bf16[32,768]{1,0:T(8,128)(2,1)} %bitcast.43, bf16[2,4,192,768]{3,2,1,0:T(8,128)(2,1)} %pad_maximum_fusion.table_ref, bf16[4,192,128]{2,1,0:T(8,128)(2,1)} %bitcast_select_fusion.ztable_ref, ...), custom_call_target="tpu_custom_call" | custom-call | tf_op jit(solution)/shard_map/pallas_call | solution.py:214
  135.3 0.8 slice_bitcast_fusion.1
  136.2 0.8 multiply_add_fusion
  136.9 7.3 %convert_bitcast_fusion = f32[192,8,4,384]{3,0,1,2:T(8,128)} fusion(bf16[4,8,192,384]{3,2,1,0:T(8,128)(2,1)} %get-tuple-element.12), kind=kLoop, calls=%fused_computation | loop fusion | flops 2359296 | bytes 14155776 | tf_op jit(solution)/shard_map/convert_element_type | solution.py:238
  144.2 13.4 %copy.5 = f32[192,8,4,384]{3,2,1,0:T(4,128)} copy(f32[192,8,4,384]{3,0,1,2:T(8,128)} %convert_bitcast_fusion) | data formatting | bytes 18874368 | tf_op jit(solution)/shard_map/convert_element_type | solution.py:238
  157.6 12.0 %reshape.305 = f32[192,8,1536]{2,1,0:T(8,128)} reshape(f32[192,8,4,384]{3,2,1,0:T(4,128)} %copy.5) | data formatting | bytes 18874368 | tf_op jit(solution)/shard_map/convert_element_type | solution.py:238
  (19 shorter events, 0.1 us)
